TPU v7x, 32 devices: a whole 2x2x4 slice. The times are simulated.
32 devices in a mesh: gx: 4 (over y, x), gy: 2 (over core), row: 4 (over z).
Axes of the slice: x: 2, y: 2, z: 4, core: 2. Of those that a mesh axis runs over, the one named last changes fastest.
Arguments:
- occupancy: int32 [32, 512, 1024], P('row', 'gx', 'gy'), may hold values 0 or 1
- random_draws: bfloat16 [4, 32, 512, 1024], P(None, 'row', 'gx', 'gy'), may hold values from 0 to 1
Outputs:
- coverage: float32 [128, 256], P('gx', 'gy')
- projected: float32 [128, 256], P('gx', 'gy')
All inputs are finite; a program needn't handle non-finite values. No bound on the sum of `occupancy` on one device may be relied on, other than what follows from the above.
Results may differ from a plain program's by a relative error of at most 0.0003.
Values may be sent and summed in bfloat16 or wider, within the bound.
No kernel may reach another device: no remote copies, remote signals or barrier semaphores. Data moves between devices by JAX's collectives and lax.ppermute only.
A program may use at most 64 MiB of HBM per device.

v0:
```python
import jax
import jax.numpy as jnp
from jax import lax
from jax.sharding import PartitionSpec as P

SWEEPS = 4
BLOCK = 4
LEAP = 8
ADSORB = 0.6
DESORB = 0.6
HOPPING = 0.3
COUPLING = 0.5


def padded_2(block, sides, width):
    for axis, dim in sides:
        count = lax.axis_size(axis)
        forward = [(i, i + 1) for i in range(count - 1)]
        forward.append((count - 1, 0))
        backward = [(target, source) for source, target in forward]
        low = lax.ppermute(
            lax.slice_in_dim(block, block.shape[dim] - width, None, axis=dim), axis, forward
        )
        high = lax.ppermute(lax.slice_in_dim(block, 0, width, axis=dim), axis, backward)
        block = jnp.concatenate([low, block, high], axis=dim)
    return block


def sublattice_update(padded, jitter, colour):
    centre = padded[..., 1:-1, 1:-1]
    beside = (
        padded[..., 2:, 1:-1]
        + padded[..., :-2, 1:-1]
        + padded[..., 1:-1, 2:]
        + padded[..., 1:-1, :-2]
    )
    updated = (
        centre
        + ADSORB * jitter * (1.0 - centre)
        - DESORB * (1.0 - jitter) * jnp.exp(-COUPLING * beside) * centre
        + HOPPING * (0.25 * beside - centre)
    )
    row_index = lax.broadcasted_iota(jnp.int32, centre.shape[-2:], 0)
    col_index = lax.broadcasted_iota(jnp.int32, centre.shape[-2:], 1)
    chosen = (row_index + col_index + colour) % 2 == 0
    return jnp.where(chosen[None], updated, centre)


def block_sums(field):
    height, width = (field.shape[-2], field.shape[-1])
    shaped = field.reshape(field.shape[:-2] + (height // BLOCK, BLOCK, width // BLOCK, BLOCK))
    return jnp.sum(shaped, axis=(-3, -1))


def per_device(occupancy, random_draws):
    occupied = occupancy.astype(jnp.float32)
    earlier = occupied
    even_draws = padded_2(random_draws[0::2], (("gx", 2), ("gy", 3)), 1)
    for pair_index in range(SWEEPS // 2):
        if 2 * pair_index == SWEEPS - 2:
            earlier = occupied
        widened = padded_2(occupied, (("gx", 1), ("gy", 2)), 2)
        middle = sublattice_update(widened, even_draws[pair_index].astype(jnp.float32), 0)
        occupied = sublattice_update(
            middle, random_draws[2 * pair_index + 1].astype(jnp.float32), 1
        )
    snapshots = jnp.stack([jnp.sum(earlier, axis=0), jnp.sum(occupied, axis=0)])
    coarse_sums = lax.psum(block_sums(snapshots), "row")
    divisor = jnp.float32(occupancy.shape[0] * lax.axis_size("row") * BLOCK * BLOCK)
    averages = coarse_sums / divisor
    coverage = averages[1]
    projected = coverage + LEAP / 2.0 * (coverage - averages[0])
    return (coverage, projected)


def solution(mesh):
    in_specs = (P("row", "gx", "gy"), P(None, "row", "gx", "gy"))
    out_specs = (P("gx", "gy"), P("gx", "gy"))
    return jax.shard_map(
        per_device, mesh=mesh, in_specs=in_specs, out_specs=out_specs, check_vma=False
    )
```

profile of v0, /device:TPU:0, one launch (start us, length us, event | category | flops | bytes accessed | tf_op | source)
XLA Modules:
  0.0 108.9 jit_solution(14045809891136270607)
XLA Ops:
  0.6 0.0 copy-start.3
  0.6 3.0 %copy_convert_fusion = f32[8,128,512]{2,0,1:T(8,128)S(1)} fusion(s32[8,128,512]{2,1,0:T(8,128)} %param.2), kind=kLoop, calls=%fused_computation.76 | loop fusion | flops 524288 | bytes 4194304 | tf_op jit(solution)/shard_map/convert_element_type | solution.py:56
  3.6 3.0 %collective-permute-start = (f32[8,2,512]{2,0,1:T(8,128)S(1)}, f32[8,2,512]{2,0,1:T(8,128)S(1)}, u32[]{:S(2)}, u32[]{:S(2)}) collective-permute-start(f32[8,2,512]{2,0,1:T(8,128)S(1)} %get-tuple-element.18), channel_id=1, source_target_pairs={{0,8},{8,16},{16,24},{24,0},{1,9},{9,17},{17,25},{25,1},{2,10},{10... | collective-permute-start | bytes 98312 | tf_op jit(solution)/shard_map/ppermute | solution.py:21
  6.6 1.0 collective-permute-start.1
  7.7 0.2 slice.126
  7.8 0.1 fusion.60
  7.9 1.1 collective-permute-start.4
  9.0 1.9 %collective-permute-start.5 = (bf16[2,8,1,512]{3,1,2,0:T(8,128)(2,1)S(1)}, bf16[2,8,1,512]{3,1,2,0:T(8,128)(2,1)S(1)}, u32[]{:S(2)}, u32[]{:S(2)}) collective-permute-start(bf16[2,8,1,512]{3,1,2,0:T(8,128)(2,1)S(1)} %copy.54), channel_id=1, source_target_pairs={{8,0},{16,8},{24,16},{0,24},{9,1},{17,9},{25,17},{1,25},{10,2},{18... | collective-permute-start | bytes 49160 | tf_op jit(solution)/shard_map/ppermute | solution.py:24
  10.9 1.5 %fusion.57 = (bf16[1,8,128,512]{3,2,1,0:T(8,128)(2,1)}, bf16[1,8,128,512]{3,2,1,0:T(8,128)(2,1)}) fusion(bf16[4,8,128,512]{3,2,1,0:T(8,128)(2,1)S(1)} %copy-done.3), kind=kLoop, calls=%fused_computation.107 | loop fusion | bytes 4194304 | tf_op jit(solution)/shard_map/slice | solution.py:65
  12.4 0.1 fusion.46
  12.5 0.1 collective-permute-done.4
  12.6 1.2 %constant_dynamic-update-slice_fusion.1 = bf16[2,8,130,512]{3,1,2,0:T(8,128)(2,1)S(1)} fusion(bf16[2,8,130,512]{3,1,2,0:T(8,128)(2,1)S(1)} %constant_dynamic-update-slice_fusion.2, bf16[2,8,128,512]{3,2,1,0:T(8,128)(2,1)S(1)} %slice.126), kind=kLoop, calls=%fused_computation.104 | loop fusion | bytes 4194304
  13.8 0.0 collective-permute-done.5
  13.8 0.0 copy-start.2
  13.8 1.3 %copy-done.2 = bf16[2,8,130,512]{3,1,2,0:T(8,128)(2,1)} copy-done((bf16[2,8,130,512]{3,1,2,0:T(8,128)(2,1)}, bf16[2,8,130,512]{3,1,2,0:T(8,128)(2,1)S(1)}, u32[]{:S(2)}) %copy-start.2) | copy-done | bytes 2129944
  15.1 0.3 fusion.58
  15.4 0.4 copy.16
  15.8 0.0 collective-permute-start.6
  15.9 0.4 copy.17
  16.3 0.5 collective-permute-start.7
  16.9 0.7 fusion.51
  17.6 0.0 collective-permute-done.6
  17.6 1.3 %copy.18 = bf16[2,8,130,1]{3,1,2,0:T(8,128)(2,1)} copy(bf16[2,8,130,1]{2,1,3,0:T(8,128)(2,1)S(1)} %collective-permute-done.6) | data formatting | bytes 8320 | tf_op jit(solution)/shard_map/ppermute | solution.py:21
  18.9 0.0 collective-permute-done.7
  18.9 1.3 %copy.19 = bf16[2,8,130,1]{3,1,2,0:T(8,128)(2,1)} copy(bf16[2,8,130,1]{2,1,3,0:T(8,128)(2,1)S(1)} %collective-permute-done.7) | data formatting | bytes 8320 | tf_op jit(solution)/shard_map/ppermute | solution.py:24
  20.1 0.0 collective-permute-done
  20.2 0.0 collective-permute-done.1
  20.2 0.2 pad_maximum_fusion.18
  20.4 0.3 copy.11
  20.7 0.1 collective-permute-start.2
  20.8 0.3 copy.12
  21.1 0.5 collective-permute-start.3
  21.6 5.0 %pad_maximum_fusion.14 = bf16[2,8,130,514]{3,1,2,0:T(8,128)(2,1)} fusion(bf16[2,8,130,1]{3,1,2,0:T(8,128)(2,1)} %copy.19, bf16[2,8,130,512]{3,1,2,0:T(8,128)(2,1)} %copy-done.2, bf16[2,8,130,1]{3,1,2,0:T(8,128)(2,1)} %copy.18), kind=kLoop, calls=%fused_computation.44 | loop fusion | flops 6414720 | bytes 4276480 | tf_op jit(solution)/shard_map/concatenate | solution.py:25
  26.6 0.0 collective-permute-done.2
  26.7 0.4 copy.13
  27.1 0.0 collective-permute-done.3
  27.1 0.4 copy.14
  27.5 0.9 pad_maximum_fusion
  28.4 0.8 copy-done
  29.2 4.2 %fusion.5 = f32[8,130,514]{2,0,1:T(8,128)S(1)} fusion(f32[8,2,512]{2,0,1:T(8,128)S(1)} %collective-permute-done.1, f32[8,128,512]{2,0,1:T(8,128)S(1)} %copy_convert_fusion, f32[8,2,512]{2,0,1:T(8,128)S(1)} %collective-permute-done, f32[8,132,2]{2,0,1:T(8,128)S(1)} %copy.13, f32[8,132,2]{2,0,1:T(8,128)S(1)} %copy.14, f32[8,132,516]{2,0,1:T(8,128)S(1)} %pad_maximum_fusion, ...), kind=kLoop, calls=%fused_computation.11 | loop fusion | flops 13364000 | bytes 11868484 | tf_op jit(solution)/shard_map/jit(_where)/select_n | solution.py:46
  33.5 4.6 %fusion.55 = (f32[128,512]{1,0:T(8,128)S(1)}, f32[8,128,512]{2,0,1:T(8,128)S(1)}) fusion(f32[8,130,514]{2,0,1:T(8,128)S(1)} %fusion.5, bf16[1,8,128,512]{3,2,1,0:T(8,128)(2,1)S(1)} %copy-done.5, pred[128,512]{1,0:T(8,128)(4,1)S(1)} %copy-done.6), kind=kLoop, calls=%fused_computation.106 | loop fusion | flops 10420224 | bytes 13959168 | tf_op jit(solution)/shard_map/reduce_sum | solution.py:67
  38.1 2.3 %collective-permute-start.8 = (f32[8,2,512]{2,0,1:T(8,128)S(1)}, f32[8,2,512]{2,0,1:T(8,128)S(1)}, u32[]{:S(2)}, u32[]{:S(2)}) collective-permute-start(f32[8,2,512]{2,0,1:T(8,128)S(1)} %get-tuple-element.14), channel_id=1, source_target_pairs={{0,8},{8,16},{16,24},{24,0},{1,9},{9,17},{17,25},{25,1},{2,10},{10... | collective-permute-start | bytes 98312 | tf_op jit(solution)/shard_map/ppermute | solution.py:21
  40.3 0.7 collective-permute-start.9
  41.1 2.0 %collective-permute-done.8 = f32[8,2,512]{2,0,1:T(8,128)S(1)} collective-permute-done((f32[8,2,512]{2,0,1:T(8,128)S(1)}, f32[8,2,512]{2,0,1:T(8,128)S(1)}, u32[]{:S(2)}, u32[]{:S(2)}) %collective-permute-start.8) | collective-permute-done | bytes 32800 | tf_op jit(solution)/shard_map/ppermute | solution.py:21
  43.1 1.2 %collective-permute-done.9 = f32[8,2,512]{2,0,1:T(8,128)S(1)} collective-permute-done((f32[8,2,512]{2,0,1:T(8,128)S(1)}, f32[8,2,512]{2,0,1:T(8,128)S(1)}, u32[]{:S(2)}, u32[]{:S(2)}) %collective-permute-start.9) | collective-permute-done | bytes 32800 | tf_op jit(solution)/shard_map/ppermute | solution.py:24
  44.3 0.2 pad_maximum_fusion.15
  44.5 0.4 copy-done.10
  44.9 0.3 copy.25
  45.2 0.1 collective-permute-start.10
  45.3 0.3 copy.26
  45.6 0.5 collective-permute-start.11
  46.2 10.0 %reshape.78 = f32[1,32,4,128,4]{4,3,2,1,0:T(8,128)} reshape(f32[128,512]{1,0:T(8,128)S(1)} %get-tuple-element.4) | data formatting | bytes 524288 | tf_op jit(solution)/shard_map/stack | solution.py:67
  56.2 5.2 %copy.34 = f32[1,32,4,128,4]{3,1,4,2,0:T(8,128)S(1)} copy(f32[1,32,4,128,4]{4,3,2,1,0:T(8,128)} %reshape.78) | data formatting | bytes 524288 | tf_op jit(solution)/shard_map/stack | solution.py:67
  61.4 0.0 collective-permute-done.10
  61.5 0.4 copy.27
  61.9 0.0 collective-permute-done.11
  61.9 1.1 %copy.28 = f32[8,132,2]{2,0,1:T(8,128)S(1)} copy(f32[8,132,2]{1,0,2:T(8,128)} %collective-permute-done.11) | data formatting | bytes 16896 | tf_op jit(solution)/shard_map/ppermute | solution.py:24
  63.0 1.8 %pad_maximum_fusion.1 = f32[8,132,516]{2,0,1:T(8,128)S(1)} fusion(f32[8,132,2]{2,0,1:T(8,128)S(1)} %copy.28, f32[8,2,512]{2,0,1:T(8,128)} %copy-done.10, f32[8,128,512]{2,0,1:T(8,128)S(1)} %get-tuple-element.5, f32[8,2,512]{2,0,1:T(8,128)} %copy-done.8, f32[8,132,2]{2,0,1:T(8,128)S(1)} %copy.27), kind=kLoop, calls=%fused_computation.5 | loop fusion | flops 2179584 | bytes 4359168 | tf_op jit(solution)/shard_map/concatenate | solution.py:25
  64.9 4.2 %fusion.15 = f32[8,130,514]{2,0,1:T(8,128)S(1)} fusion(f32[8,2,512]{2,0,1:T(8,128)S(1)} %copy-done.11, f32[8,128,512]{2,0,1:T(8,128)S(1)} %get-tuple-element.5, f32[8,2,512]{2,0,1:T(8,128)S(1)} %copy-done.9, f32[8,132,2]{2,0,1:T(8,128)S(1)} %copy.27, f32[8,132,2]{2,0,1:T(8,128)S(1)} %copy.28, f32[8,132,516]{2,0,1:T(8,128)S(1)} %pad_maximum_fusion.1, ...), kind=kLoop, calls=%fused_computation.21 | loop fusion | flops 13364000 | bytes 11868484 | tf_op jit(solution)/shard_map/jit(_where)/select_n | solution.py:46
  69.2 4.5 %fusion.40 = f32[128,512]{1,0:T(8,128)S(1)} fusion(f32[8,130,514]{2,0,1:T(8,128)S(1)} %fusion.15, bf16[1,8,128,512]{3,2,1,0:T(8,128)(2,1)S(1)} %copy-done.4, pred[128,512]{1,0:T(8,128)(4,1)S(1)} %copy-done.7), kind=kLoop, calls=%fused_computation.65 | loop fusion | flops 10420224 | bytes 11862016 | tf_op jit(solution)/shard_map/reduce_sum | solution.py:67
  73.7 10.0 %reshape.79 = f32[1,32,4,128,4]{4,3,2,1,0:T(8,128)} reshape(f32[128,512]{1,0:T(8,128)S(1)} %fusion.40) | data formatting | bytes 524288 | tf_op jit(solution)/shard_map/stack | solution.py:67
  83.7 5.2 %copy.35 = f32[1,32,4,128,4]{3,1,4,2,0:T(8,128)S(1)} copy(f32[1,32,4,128,4]{4,3,2,1,0:T(8,128)} %reshape.79) | data formatting | bytes 524288 | tf_op jit(solution)/shard_map/stack | solution.py:67
  89.0 19.3 %psum.7 = f32[2,32,128]{2,1,0:T(8,128)S(1)} all-reduce(f32[2,32,128]{2,1,0:T(8,128)S(1)} %maximum_reduce_fusion), channel_id=1, replica_groups=mesh['gx'=4,'gy'=2,'row'=4] {'row'}, use_global_device_ids=true, to_apply=%region_3.4 | all-reduce | flops 8192 | bytes 65536 | tf_op jit(solution)/shard_map/psum | solution.py:68
  108.3 0.6 fusion.54
  (27 shorter events, 0.1 us)
Async XLA Ops:
  0.6 7.0 %copy-start.3 = (bf16[4,8,128,512]{3,2,1,0:T(8,128)(2,1)S(1)}, bf16[4,8,128,512]{3,2,1,0:T(8,128)(2,1)}, u32[]{:S(2)}) copy-start(bf16[4,8,128,512]{3,2,1,0:T(8,128)(2,1)} %param.3) | copy-start | bytes 12582916
  3.6 16.5 %collective-permute-start = (f32[8,2,512]{2,0,1:T(8,128)S(1)}, f32[8,2,512]{2,0,1:T(8,128)S(1)}, u32[]{:S(2)}, u32[]{:S(2)}) collective-permute-start(f32[8,2,512]{2,0,1:T(8,128)S(1)} %get-tuple-element.18), channel_id=1, source_target_pairs={{0,8},{8,16},{16,24},{24,0},{1,9},{9,17},{17,25},{25,1},{2,10},{10... | collective-permute-start | bytes 98312 | tf_op jit(solution)/shard_map/ppermute | solution.py:21
  6.6 13.5 %collective-permute-start.1 = (f32[8,2,512]{2,0,1:T(8,128)S(1)}, f32[8,2,512]{2,0,1:T(8,128)S(1)}, u32[]{:S(2)}, u32[]{:S(2)}) collective-permute-start(f32[8,2,512]{2,0,1:T(8,128)S(1)} %get-tuple-element.19), channel_id=1, source_target_pairs={{8,0},{16,8},{24,16},{0,24},{9,1},{17,9},{25,17},{1,25},{10,2},{18... | collective-permute-start | bytes 98312 | tf_op jit(solution)/shard_map/ppermute | solution.py:24
  7.9 4.7 %collective-permute-start.4 = (bf16[2,8,1,512]{3,1,2,0:T(8,128)(2,1)S(1)}, bf16[2,8,1,512]{3,1,2,0:T(8,128)(2,1)S(1)}, u32[]{:S(2)}, u32[]{:S(2)}) collective-permute-start(bf16[2,8,1,512]{3,1,2,0:T(8,128)(2,1)S(1)} %copy.53), channel_id=1, source_target_pairs={{0,8},{8,16},{16,24},{24,0},{1,9},{9,17},{17,25},{25,1},{2,10},{10... | collective-permute-start | bytes 49160 | tf_op jit(solution)/shard_map/ppermute | solution.py:21
  9.0 4.8 %collective-permute-start.5 = (bf16[2,8,1,512]{3,1,2,0:T(8,128)(2,1)S(1)}, bf16[2,8,1,512]{3,1,2,0:T(8,128)(2,1)S(1)}, u32[]{:S(2)}, u32[]{:S(2)}) collective-permute-start(bf16[2,8,1,512]{3,1,2,0:T(8,128)(2,1)S(1)} %copy.54), channel_id=1, source_target_pairs={{8,0},{16,8},{24,16},{0,24},{9,1},{17,9},{25,17},{1,25},{10,2},{18... | collective-permute-start | bytes 49160 | tf_op jit(solution)/shard_map/ppermute | solution.py:24
  13.8 1.3 %copy-start.2 = (bf16[2,8,130,512]{3,1,2,0:T(8,128)(2,1)}, bf16[2,8,130,512]{3,1,2,0:T(8,128)(2,1)S(1)}, u32[]{:S(2)}) copy-start(bf16[2,8,130,512]{3,1,2,0:T(8,128)(2,1)S(1)} %constant_dynamic-update-slice_fusion) | copy-start | bytes 6389764
  15.8 1.8 %collective-permute-start.6 = (bf16[2,8,130,1]{2,1,3,0:T(8,128)(2,1)S(1)}, bf16[2,8,130,1]{2,1,3,0:T(8,128)(2,1)S(1)}, u32[]{:S(2)}, u32[]{:S(2)}) collective-permute-start(bf16[2,8,130,1]{2,1,3,0:T(8,128)(2,1)S(1)} %copy.16), channel_id=1, source_target_pairs={{0,4},{4,0},{1,5},{5,1},{2,6},{6,2},{3,7},{7,3},{8,12},{12,8},{9,1... | collective-permute-start | bytes 12488 | tf_op jit(solution)/shard_map/ppermute | solution.py:21
  16.3 2.5 %collective-permute-start.7 = (bf16[2,8,130,1]{2,1,3,0:T(8,128)(2,1)S(1)}, bf16[2,8,130,1]{2,1,3,0:T(8,128)(2,1)S(1)}, u32[]{:S(2)}, u32[]{:S(2)}) collective-permute-start(bf16[2,8,130,1]{2,1,3,0:T(8,128)(2,1)S(1)} %copy.17), channel_id=1, source_target_pairs={{4,0},{0,4},{5,1},{1,5},{6,2},{2,6},{7,3},{3,7},{12,8},{8,12},{13,... | collective-permute-start | bytes 12488 | tf_op jit(solution)/shard_map/ppermute | solution.py:24
  20.7 6.0 %collective-permute-start.2 = (f32[8,132,2]{1,0,2:T(8,128)S(1)}, f32[8,132,2]{1,0,2:T(8,128)S(1)}, u32[]{:S(2)}, u32[]{:S(2)}) collective-permute-start(f32[8,132,2]{1,0,2:T(8,128)S(1)} %copy.11), channel_id=1, source_target_pairs={{0,4},{4,0},{1,5},{5,1},{2,6},{6,2},{3,7},{7,3},{8,12},{12,8},{9,1... | collective-permute-start | bytes 25352 | tf_op jit(solution)/shard_map/ppermute | solution.py:21
  21.1 6.0 %collective-permute-start.3 = (f32[8,132,2]{1,0,2:T(8,128)S(1)}, f32[8,132,2]{1,0,2:T(8,128)S(1)}, u32[]{:S(2)}, u32[]{:S(2)}) collective-permute-start(f32[8,132,2]{1,0,2:T(8,128)S(1)} %copy.12), channel_id=1, source_target_pairs={{4,0},{0,4},{5,1},{1,5},{6,2},{2,6},{7,3},{3,7},{12,8},{8,12},{13,... | collective-permute-start | bytes 25352 | tf_op jit(solution)/shard_map/ppermute | solution.py:24
  27.5 1.8 %copy-start = (bf16[2,8,130,514]{3,1,2,0:T(8,128)(2,1)S(1)}, bf16[2,8,130,514]{3,1,2,0:T(8,128)(2,1)}, u32[]{:S(2)}) copy-start(bf16[2,8,130,514]{3,1,2,0:T(8,128)(2,1)} %pad_maximum_fusion.14) | copy-start | bytes 6414724
  29.2 4.2 %copy-start.5 = (bf16[1,8,128,512]{3,2,1,0:T(8,128)(2,1)S(1)}, bf16[1,8,128,512]{3,2,1,0:T(8,128)(2,1)}, u32[]{:S(2)}) copy-start(bf16[1,8,128,512]{3,2,1,0:T(8,128)(2,1)} %get-tuple-element.7) | copy-start | bytes 3145732
  29.2 4.2 %copy-start.6 = (pred[128,512]{1,0:T(8,128)(4,1)S(1)}, pred[128,512]{1,0:T(8,128)(4,1)}, u32[]{:S(2)}) copy-start(pred[128,512]{1,0:T(8,128)(4,1)} %fusion.51) | copy-start | bytes 196612
  38.1 5.0 %collective-permute-start.8 = (f32[8,2,512]{2,0,1:T(8,128)S(1)}, f32[8,2,512]{2,0,1:T(8,128)S(1)}, u32[]{:S(2)}, u32[]{:S(2)}) collective-permute-start(f32[8,2,512]{2,0,1:T(8,128)S(1)} %get-tuple-element.14), channel_id=1, source_target_pairs={{0,8},{8,16},{16,24},{24,0},{1,9},{9,17},{17,25},{25,1},{2,10},{10... | collective-permute-start | bytes 98312 | tf_op jit(solution)/shard_map/ppermute | solution.py:21
  40.3 3.9 %collective-permute-start.9 = (f32[8,2,512]{2,0,1:T(8,128)S(1)}, f32[8,2,512]{2,0,1:T(8,128)S(1)}, u32[]{:S(2)}, u32[]{:S(2)}) collective-permute-start(f32[8,2,512]{2,0,1:T(8,128)S(1)} %get-tuple-element.15), channel_id=1, source_target_pairs={{8,0},{16,8},{24,16},{0,24},{9,1},{17,9},{25,17},{1,25},{10,2},{18... | collective-permute-start | bytes 98312 | tf_op jit(solution)/shard_map/ppermute | solution.py:24
  43.1 1.2 %copy-start.8 = (f32[8,2,512]{2,0,1:T(8,128)}, f32[8,2,512]{2,0,1:T(8,128)S(1)}, u32[]{:S(2)}) copy-start(f32[8,2,512]{2,0,1:T(8,128)S(1)} %collective-permute-done.8) | copy-start | bytes 98308
  44.3 0.6 copy-start.10
  45.2 16.2 %collective-permute-start.10 = (f32[8,132,2]{1,0,2:T(8,128)S(1)}, f32[8,132,2]{1,0,2:T(8,128)S(1)}, u32[]{:S(2)}, u32[]{:S(2)}) collective-permute-start(f32[8,132,2]{1,0,2:T(8,128)S(1)} %copy.25), channel_id=1, source_target_pairs={{0,4},{4,0},{1,5},{5,1},{2,6},{6,2},{3,7},{7,3},{8,12},{12,8},{9,1... | collective-permute-start | bytes 25352 | tf_op jit(solution)/shard_map/ppermute | solution.py:21
  45.6 16.2 %collective-permute-start.11 = (f32[8,132,2]{1,0,2:T(8,128)S(1)}, f32[8,132,2]{1,0,2:T(8,128)}, u32[]{:S(2)}, u32[]{:S(2)}) collective-permute-start(f32[8,132,2]{1,0,2:T(8,128)S(1)} %copy.26), channel_id=1, source_target_pairs={{4,0},{0,4},{5,1},{1,5},{6,2},{2,6},{7,3},{3,7},{12,8},{8,12},{13,... | collective-permute-start | bytes 25352 | tf_op jit(solution)/shard_map/ppermute | solution.py:24
  63.0 1.9 %copy-start.1 = (bf16[2,8,130,514]{3,1,2,0:T(8,128)(2,1)S(1)}, bf16[2,8,130,514]{3,1,2,0:T(8,128)(2,1)}, u32[]{:S(2)}) copy-start(bf16[2,8,130,514]{3,1,2,0:T(8,128)(2,1)} %pad_maximum_fusion.14) | copy-start | bytes 6414724
  63.0 1.9 %copy-start.9 = (f32[8,2,512]{2,0,1:T(8,128)S(1)}, f32[8,2,512]{2,0,1:T(8,128)}, u32[]{:S(2)}) copy-start(f32[8,2,512]{2,0,1:T(8,128)} %copy-done.8) | copy-start | bytes 98308
  63.0 1.9 %copy-start.11 = (f32[8,2,512]{2,0,1:T(8,128)S(1)}, f32[8,2,512]{2,0,1:T(8,128)}, u32[]{:S(2)}) copy-start(f32[8,2,512]{2,0,1:T(8,128)} %copy-done.10) | copy-start | bytes 98308
  64.9 4.3 %copy-start.4 = (bf16[1,8,128,512]{3,2,1,0:T(8,128)(2,1)S(1)}, bf16[1,8,128,512]{3,2,1,0:T(8,128)(2,1)}, u32[]{:S(2)}) copy-start(bf16[1,8,128,512]{3,2,1,0:T(8,128)(2,1)} %get-tuple-element.6) | copy-start | bytes 3145732
  64.9 4.3 %copy-start.7 = (pred[128,512]{1,0:T(8,128)(4,1)S(1)}, pred[128,512]{1,0:T(8,128)(4,1)}, u32[]{:S(2)}) copy-start(pred[128,512]{1,0:T(8,128)(4,1)} %fusion.51) | copy-start | bytes 196612
where the time goes:
time: 109 us
  local copies, waits for them, and re-layouts  43.4 us (40%)
  other arithmetic  30.1 us (28%)
  blocking collectives  19.3 us (18%)
  starting transfers between devices  11.8 us (11%)
  waiting for transfers between devices  3.33 us (3%)
    another operation x4, local copies, waits for them, and re-layouts, per_device(): snapshots = jnp.stack([jnp.sum(earlier, axis=0), jnp.sum(occupied, axis=0)])  30.5 us
    psum x1, blocking collectives, per_device(): coarse_sums = lax.psum(block_sums(snapshots), 'row')  19.3 us
    reduce_sum x2, other arithmetic, per_device(): snapshots = jnp.stack([jnp.sum(earlier, axis=0), jnp.sum(occupied, axis=0)])  9.11 us
    select_n x2, other arithmetic, sublattice_update(): return jnp.where(chosen[None], updated, centre)  8.46 us
    concatenate x5, other arithmetic, padded_2(): block = jnp.concatenate([low, block, high], axis=dim)  8.14 us
    ppermute x6, starting transfers between devices, padded_2(): lax.ppermute(lax.slice_in_dim(block, block.shape[dim] - width, None, axis...  6.51 us
    ppermute x6, starting transfers between devices, padded_2(): lax.ppermute(lax.slice_in_dim(block, 0, width, axis=dim), axis, backward)  5.3 us
    unnamed x28, local copies, waits for them, and re-layouts  3.81 us
  transfers between devices with their start and end apart: 12, of which 3 were waited for; matrix products, arithmetic and copies ran while one was open for 27% of the time, Pallas kernels for 0%

commit v1 on v0

--- a/solution.py
+++ b/solution.py
@@ -65,7 +65,9 @@
             middle, random_draws[2 * pair_index + 1].astype(jnp.float32), 1
         )
     snapshots = jnp.stack([jnp.sum(earlier, axis=0), jnp.sum(occupied, axis=0)])
-    coarse_sums = lax.psum(block_sums(snapshots), "row")
+    point = block_sums(snapshots)
+    placed = lax.all_gather(point, "row")
+    coarse_sums = jnp.sum(placed, 0)
     divisor = jnp.float32(occupancy.shape[0] * lax.axis_size("row") * BLOCK * BLOCK)
     averages = coarse_sums / divisor
     coverage = averages[1]

time: 109 us -> 104 us (0.954)
  blocking collectives: 19.3 us -> 13.6 us
    psum x1 -> x0, blocking collectives: 19.3 us -> none  [per_device(): coarse_sums = lax.psum(block_sums(snapshots), 'row')]
    all_gather x0 -> x1, blocking collectives: none -> 13.6 us  [per_device(): placed = lax.all_gather(point, 'row')]
  transfers between devices with their start and end apart: 12 -> 12, of which waited for: 3 -> 3; matrix products, arithmetic and copies ran while one was open for 27% -> 28% of each run, Pallas kernels for 0% -> 0%
where the time goes in v1:
time: 104 us; the launch traced here: 103 us
  local copies, waits for them, and re-layouts  43.4 us (42%)
  other arithmetic  30.2 us (29%)
  blocking collectives  13.6 us (13%)
  starting transfers between devices  11.8 us (11%)
  waiting for transfers between devices  3.33 us (3%)
    another operation x4, local copies, waits for them, and re-layouts, per_device(): snapshots = jnp.stack([jnp.sum(earlier, axis=0), jnp.sum(occupied, axis=0)])  30.5 us
    all_gather x1, blocking collectives, per_device(): placed = lax.all_gather(point, 'row')  13.6 us
    reduce_sum x2, other arithmetic, per_device(): snapshots = jnp.stack([jnp.sum(earlier, axis=0), jnp.sum(occupied, axis=0)])  9.11 us
    select_n x2, other arithmetic, sublattice_update(): return jnp.where(chosen[None], updated, centre)  8.46 us
    concatenate x5, other arithmetic, padded_2(): block = jnp.concatenate([low, block, high], axis=dim)  8.14 us
    ppermute x6, starting transfers between devices, padded_2(): lax.ppermute(lax.slice_in_dim(block, block.shape[dim] - width, None, axis...  6.51 us
    ppermute x6, starting transfers between devices, padded_2(): lax.ppermute(lax.slice_in_dim(block, 0, width, axis=dim), axis, backward)  5.3 us
    unnamed x28, local copies, waits for them, and re-layouts  3.81 us
  transfers between devices with their start and end apart: 12, of which 3 were waited for; matrix products, arithmetic and copies ran while one was open for 28% of the time, Pallas kernels for 0%

profile of v1, /device:TPU:0, one launch (start us, length us, event | category | flops | bytes accessed | tf_op | source)
XLA Modules:
  0.0 103.3 jit_solution(14946772880536103160)
XLA Ops:
  0.6 0.0 copy-start.3
  0.6 3.0 %copy_convert_fusion = f32[8,128,512]{2,0,1:T(8,128)S(1)} fusion(s32[8,128,512]{2,1,0:T(8,128)} %param.2), kind=kLoop, calls=%fused_computation.76 | loop fusion | flops 524288 | bytes 4194304 | tf_op jit(solution)/shard_map/convert_element_type | solution.py:56
  3.6 3.0 %collective-permute-start = (f32[8,2,512]{2,0,1:T(8,128)S(1)}, f32[8,2,512]{2,0,1:T(8,128)S(1)}, u32[]{:S(2)}, u32[]{:S(2)}) collective-permute-start(f32[8,2,512]{2,0,1:T(8,128)S(1)} %get-tuple-element.18), channel_id=1, source_target_pairs={{0,8},{8,16},{16,24},{24,0},{1,9},{9,17},{17,25},{25,1},{2,10},{10... | collective-permute-start | bytes 98312 | tf_op jit(solution)/shard_map/ppermute | solution.py:21
  6.6 1.0 collective-permute-start.1
  7.7 0.2 slice.126
  7.8 0.1 fusion.60
  7.9 1.1 %collective-permute-start.4 = (bf16[2,8,1,512]{3,1,2,0:T(8,128)(2,1)S(1)}, bf16[2,8,1,512]{3,1,2,0:T(8,128)(2,1)S(1)}, u32[]{:S(2)}, u32[]{:S(2)}) collective-permute-start(bf16[2,8,1,512]{3,1,2,0:T(8,128)(2,1)S(1)} %copy.53), channel_id=1, source_target_pairs={{0,8},{8,16},{16,24},{24,0},{1,9},{9,17},{17,25},{25,1},{2,10},{10... | collective-permute-start | bytes 49160 | tf_op jit(solution)/shard_map/ppermute | solution.py:21
  9.0 1.9 %collective-permute-start.5 = (bf16[2,8,1,512]{3,1,2,0:T(8,128)(2,1)S(1)}, bf16[2,8,1,512]{3,1,2,0:T(8,128)(2,1)S(1)}, u32[]{:S(2)}, u32[]{:S(2)}) collective-permute-start(bf16[2,8,1,512]{3,1,2,0:T(8,128)(2,1)S(1)} %copy.54), channel_id=1, source_target_pairs={{8,0},{16,8},{24,16},{0,24},{9,1},{17,9},{25,17},{1,25},{10,2},{18... | collective-permute-start | bytes 49160 | tf_op jit(solution)/shard_map/ppermute | solution.py:24
  10.9 1.5 %fusion.57 = (bf16[1,8,128,512]{3,2,1,0:T(8,128)(2,1)}, bf16[1,8,128,512]{3,2,1,0:T(8,128)(2,1)}) fusion(bf16[4,8,128,512]{3,2,1,0:T(8,128)(2,1)S(1)} %copy-done.3), kind=kLoop, calls=%fused_computation.107 | loop fusion | bytes 4194304 | tf_op jit(solution)/shard_map/slice | solution.py:65
  12.4 0.1 fusion.46
  12.5 0.1 collective-permute-done.4
  12.6 1.2 %constant_dynamic-update-slice_fusion.1 = bf16[2,8,130,512]{3,1,2,0:T(8,128)(2,1)S(1)} fusion(bf16[2,8,130,512]{3,1,2,0:T(8,128)(2,1)S(1)} %constant_dynamic-update-slice_fusion.2, bf16[2,8,128,512]{3,2,1,0:T(8,128)(2,1)S(1)} %slice.126), kind=kLoop, calls=%fused_computation.104 | loop fusion | bytes 4194304
  13.8 0.0 collective-permute-done.5
  13.8 0.0 copy-start.2
  13.8 1.3 %copy-done.2 = bf16[2,8,130,512]{3,1,2,0:T(8,128)(2,1)} copy-done((bf16[2,8,130,512]{3,1,2,0:T(8,128)(2,1)}, bf16[2,8,130,512]{3,1,2,0:T(8,128)(2,1)S(1)}, u32[]{:S(2)}) %copy-start.2) | copy-done | bytes 2129944
  15.1 0.3 fusion.58
  15.4 0.4 copy.16
  15.8 0.0 collective-permute-start.6
  15.9 0.4 copy.17
  16.3 0.5 collective-permute-start.7
  16.9 0.7 fusion.51
  17.6 0.0 collective-permute-done.6
  17.6 1.3 %copy.18 = bf16[2,8,130,1]{3,1,2,0:T(8,128)(2,1)} copy(bf16[2,8,130,1]{2,1,3,0:T(8,128)(2,1)S(1)} %collective-permute-done.6) | data formatting | bytes 8320 | tf_op jit(solution)/shard_map/ppermute | solution.py:21
  18.9 0.0 collective-permute-done.7
  18.9 1.3 %copy.19 = bf16[2,8,130,1]{3,1,2,0:T(8,128)(2,1)} copy(bf16[2,8,130,1]{2,1,3,0:T(8,128)(2,1)S(1)} %collective-permute-done.7) | data formatting | bytes 8320 | tf_op jit(solution)/shard_map/ppermute | solution.py:24
  20.1 0.0 collective-permute-done
  20.2 0.0 collective-permute-done.1
  20.2 0.2 pad_maximum_fusion.18
  20.4 0.3 copy.11
  20.7 0.1 collective-permute-start.2
  20.8 0.3 copy.12
  21.1 0.5 collective-permute-start.3
  21.6 5.0 %pad_maximum_fusion.14 = bf16[2,8,130,514]{3,1,2,0:T(8,128)(2,1)} fusion(bf16[2,8,130,1]{3,1,2,0:T(8,128)(2,1)} %copy.19, bf16[2,8,130,512]{3,1,2,0:T(8,128)(2,1)} %copy-done.2, bf16[2,8,130,1]{3,1,2,0:T(8,128)(2,1)} %copy.18), kind=kLoop, calls=%fused_computation.44 | loop fusion | flops 6414720 | bytes 4276480 | tf_op jit(solution)/shard_map/concatenate | solution.py:25
  26.6 0.0 collective-permute-done.2
  26.7 0.4 copy.13
  27.1 0.0 collective-permute-done.3
  27.1 0.4 copy.14
  27.5 0.9 pad_maximum_fusion
  28.4 0.8 copy-done
  29.2 4.2 %fusion.5 = f32[8,130,514]{2,0,1:T(8,128)S(1)} fusion(f32[8,2,512]{2,0,1:T(8,128)S(1)} %collective-permute-done.1, f32[8,128,512]{2,0,1:T(8,128)S(1)} %copy_convert_fusion, f32[8,2,512]{2,0,1:T(8,128)S(1)} %collective-permute-done, f32[8,132,2]{2,0,1:T(8,128)S(1)} %copy.13, f32[8,132,2]{2,0,1:T(8,128)S(1)} %copy.14, f32[8,132,516]{2,0,1:T(8,128)S(1)} %pad_maximum_fusion, ...), kind=kLoop, calls=%fused_computation.11 | loop fusion | flops 13364000 | bytes 11868484 | tf_op jit(solution)/shard_map/jit(_where)/select_n | solution.py:46
  33.5 4.6 %fusion.55 = (f32[128,512]{1,0:T(8,128)S(1)}, f32[8,128,512]{2,0,1:T(8,128)S(1)}) fusion(f32[8,130,514]{2,0,1:T(8,128)S(1)} %fusion.5, bf16[1,8,128,512]{3,2,1,0:T(8,128)(2,1)S(1)} %copy-done.5, pred[128,512]{1,0:T(8,128)(4,1)S(1)} %copy-done.6), kind=kLoop, calls=%fused_computation.106 | loop fusion | flops 10420224 | bytes 13959168 | tf_op jit(solution)/shard_map/reduce_sum | solution.py:67
  38.1 2.3 %collective-permute-start.8 = (f32[8,2,512]{2,0,1:T(8,128)S(1)}, f32[8,2,512]{2,0,1:T(8,128)S(1)}, u32[]{:S(2)}, u32[]{:S(2)}) collective-permute-start(f32[8,2,512]{2,0,1:T(8,128)S(1)} %get-tuple-element.14), channel_id=1, source_target_pairs={{0,8},{8,16},{16,24},{24,0},{1,9},{9,17},{17,25},{25,1},{2,10},{10... | collective-permute-start | bytes 98312 | tf_op jit(solution)/shard_map/ppermute | solution.py:21
  40.3 0.7 collective-permute-start.9
  41.1 2.0 %collective-permute-done.8 = f32[8,2,512]{2,0,1:T(8,128)S(1)} collective-permute-done((f32[8,2,512]{2,0,1:T(8,128)S(1)}, f32[8,2,512]{2,0,1:T(8,128)S(1)}, u32[]{:S(2)}, u32[]{:S(2)}) %collective-permute-start.8) | collective-permute-done | bytes 32800 | tf_op jit(solution)/shard_map/ppermute | solution.py:21
  43.1 1.2 %collective-permute-done.9 = f32[8,2,512]{2,0,1:T(8,128)S(1)} collective-permute-done((f32[8,2,512]{2,0,1:T(8,128)S(1)}, f32[8,2,512]{2,0,1:T(8,128)S(1)}, u32[]{:S(2)}, u32[]{:S(2)}) %collective-permute-start.9) | collective-permute-done | bytes 32800 | tf_op jit(solution)/shard_map/ppermute | solution.py:24
  44.3 0.2 pad_maximum_fusion.15
  44.5 0.4 copy-done.10
  44.9 0.3 copy.25
  45.2 0.1 collective-permute-start.10
  45.3 0.3 copy.26
  45.6 0.5 collective-permute-start.11
  46.2 10.0 %reshape.79 = f32[1,32,4,128,4]{4,3,2,1,0:T(8,128)} reshape(f32[128,512]{1,0:T(8,128)S(1)} %get-tuple-element.4) | data formatting | bytes 524288 | tf_op jit(solution)/shard_map/stack | solution.py:67
  56.2 5.2 %copy.34 = f32[1,32,4,128,4]{3,1,4,2,0:T(8,128)S(1)} copy(f32[1,32,4,128,4]{4,3,2,1,0:T(8,128)} %reshape.79) | data formatting | bytes 524288 | tf_op jit(solution)/shard_map/stack | solution.py:67
  61.4 0.0 collective-permute-done.10
  61.5 0.4 copy.27
  61.9 0.0 collective-permute-done.11
  61.9 1.1 %copy.28 = f32[8,132,2]{2,0,1:T(8,128)S(1)} copy(f32[8,132,2]{1,0,2:T(8,128)} %collective-permute-done.11) | data formatting | bytes 16896 | tf_op jit(solution)/shard_map/ppermute | solution.py:24
  63.0 1.8 %pad_maximum_fusion.1 = f32[8,132,516]{2,0,1:T(8,128)S(1)} fusion(f32[8,132,2]{2,0,1:T(8,128)S(1)} %copy.28, f32[8,2,512]{2,0,1:T(8,128)} %copy-done.10, f32[8,128,512]{2,0,1:T(8,128)S(1)} %get-tuple-element.5, f32[8,2,512]{2,0,1:T(8,128)} %copy-done.8, f32[8,132,2]{2,0,1:T(8,128)S(1)} %copy.27), kind=kLoop, calls=%fused_computation.5 | loop fusion | flops 2179584 | bytes 4359168 | tf_op jit(solution)/shard_map/concatenate | solution.py:25
  64.9 4.2 %fusion.15 = f32[8,130,514]{2,0,1:T(8,128)S(1)} fusion(f32[8,2,512]{2,0,1:T(8,128)S(1)} %copy-done.11, f32[8,128,512]{2,0,1:T(8,128)S(1)} %get-tuple-element.5, f32[8,2,512]{2,0,1:T(8,128)S(1)} %copy-done.9, f32[8,132,2]{2,0,1:T(8,128)S(1)} %copy.27, f32[8,132,2]{2,0,1:T(8,128)S(1)} %copy.28, f32[8,132,516]{2,0,1:T(8,128)S(1)} %pad_maximum_fusion.1, ...), kind=kLoop, calls=%fused_computation.21 | loop fusion | flops 13364000 | bytes 11868484 | tf_op jit(solution)/shard_map/jit(_where)/select_n | solution.py:46
  69.2 4.5 %fusion.40 = f32[128,512]{1,0:T(8,128)S(1)} fusion(f32[8,130,514]{2,0,1:T(8,128)S(1)} %fusion.15, bf16[1,8,128,512]{3,2,1,0:T(8,128)(2,1)S(1)} %copy-done.4, pred[128,512]{1,0:T(8,128)(4,1)S(1)} %copy-done.7), kind=kLoop, calls=%fused_computation.65 | loop fusion | flops 10420224 | bytes 11862016 | tf_op jit(solution)/shard_map/reduce_sum | solution.py:67
  73.7 10.0 %reshape.80 = f32[1,32,4,128,4]{4,3,2,1,0:T(8,128)} reshape(f32[128,512]{1,0:T(8,128)S(1)} %fusion.40) | data formatting | bytes 524288 | tf_op jit(solution)/shard_map/stack | solution.py:67
  83.7 5.2 %copy.35 = f32[1,32,4,128,4]{3,1,4,2,0:T(8,128)S(1)} copy(f32[1,32,4,128,4]{4,3,2,1,0:T(8,128)} %reshape.80) | data formatting | bytes 524288 | tf_op jit(solution)/shard_map/stack | solution.py:67
  89.0 13.6 %all-gather = f32[8,32,128]{2,1,0:T(8,128)S(1)} all-gather(f32[2,32,128]{2,1,0:T(8,128)S(1)} %maximum_reduce_fusion), channel_id=2, replica_groups=mesh['gx'=4,'gy'=2,'row'=4] {'row'}, dimensions={0}, use_global_device_ids=true | all-gather | bytes 163840 | tf_op jit(solution)/shard_map/all_gather | solution.py:69
  102.6 0.6 fusion.54
  (28 shorter events, 0.1 us)
Async XLA Ops:
  0.6 7.0 %copy-start.3 = (bf16[4,8,128,512]{3,2,1,0:T(8,128)(2,1)S(1)}, bf16[4,8,128,512]{3,2,1,0:T(8,128)(2,1)}, u32[]{:S(2)}) copy-start(bf16[4,8,128,512]{3,2,1,0:T(8,128)(2,1)} %param.3) | copy-start | bytes 12582916
  3.6 16.5 %collective-permute-start = (f32[8,2,512]{2,0,1:T(8,128)S(1)}, f32[8,2,512]{2,0,1:T(8,128)S(1)}, u32[]{:S(2)}, u32[]{:S(2)}) collective-permute-start(f32[8,2,512]{2,0,1:T(8,128)S(1)} %get-tuple-element.18), channel_id=1, source_target_pairs={{0,8},{8,16},{16,24},{24,0},{1,9},{9,17},{17,25},{25,1},{2,10},{10... | collective-permute-start | bytes 98312 | tf_op jit(solution)/shard_map/ppermute | solution.py:21
  6.6 13.5 %collective-permute-start.1 = (f32[8,2,512]{2,0,1:T(8,128)S(1)}, f32[8,2,512]{2,0,1:T(8,128)S(1)}, u32[]{:S(2)}, u32[]{:S(2)}) collective-permute-start(f32[8,2,512]{2,0,1:T(8,128)S(1)} %get-tuple-element.19), channel_id=1, source_target_pairs={{8,0},{16,8},{24,16},{0,24},{9,1},{17,9},{25,17},{1,25},{10,2},{18... | collective-permute-start | bytes 98312 | tf_op jit(solution)/shard_map/ppermute | solution.py:24
  7.9 4.7 %collective-permute-start.4 = (bf16[2,8,1,512]{3,1,2,0:T(8,128)(2,1)S(1)}, bf16[2,8,1,512]{3,1,2,0:T(8,128)(2,1)S(1)}, u32[]{:S(2)}, u32[]{:S(2)}) collective-permute-start(bf16[2,8,1,512]{3,1,2,0:T(8,128)(2,1)S(1)} %copy.53), channel_id=1, source_target_pairs={{0,8},{8,16},{16,24},{24,0},{1,9},{9,17},{17,25},{25,1},{2,10},{10... | collective-permute-start | bytes 49160 | tf_op jit(solution)/shard_map/ppermute | solution.py:21
  9.0 4.8 %collective-permute-start.5 = (bf16[2,8,1,512]{3,1,2,0:T(8,128)(2,1)S(1)}, bf16[2,8,1,512]{3,1,2,0:T(8,128)(2,1)S(1)}, u32[]{:S(2)}, u32[]{:S(2)}) collective-permute-start(bf16[2,8,1,512]{3,1,2,0:T(8,128)(2,1)S(1)} %copy.54), channel_id=1, source_target_pairs={{8,0},{16,8},{24,16},{0,24},{9,1},{17,9},{25,17},{1,25},{10,2},{18... | collective-permute-start | bytes 49160 | tf_op jit(solution)/shard_map/ppermute | solution.py:24
  13.8 1.3 %copy-start.2 = (bf16[2,8,130,512]{3,1,2,0:T(8,128)(2,1)}, bf16[2,8,130,512]{3,1,2,0:T(8,128)(2,1)S(1)}, u32[]{:S(2)}) copy-start(bf16[2,8,130,512]{3,1,2,0:T(8,128)(2,1)S(1)} %constant_dynamic-update-slice_fusion) | copy-start | bytes 6389764
  15.8 1.8 %collective-permute-start.6 = (bf16[2,8,130,1]{2,1,3,0:T(8,128)(2,1)S(1)}, bf16[2,8,130,1]{2,1,3,0:T(8,128)(2,1)S(1)}, u32[]{:S(2)}, u32[]{:S(2)}) collective-permute-start(bf16[2,8,130,1]{2,1,3,0:T(8,128)(2,1)S(1)} %copy.16), channel_id=1, source_target_pairs={{0,4},{4,0},{1,5},{5,1},{2,6},{6,2},{3,7},{7,3},{8,12},{12,8},{9,1... | collective-permute-start | bytes 12488 | tf_op jit(solution)/shard_map/ppermute | solution.py:21
  16.3 2.5 %collective-permute-start.7 = (bf16[2,8,130,1]{2,1,3,0:T(8,128)(2,1)S(1)}, bf16[2,8,130,1]{2,1,3,0:T(8,128)(2,1)S(1)}, u32[]{:S(2)}, u32[]{:S(2)}) collective-permute-start(bf16[2,8,130,1]{2,1,3,0:T(8,128)(2,1)S(1)} %copy.17), channel_id=1, source_target_pairs={{4,0},{0,4},{5,1},{1,5},{6,2},{2,6},{7,3},{3,7},{12,8},{8,12},{13,... | collective-permute-start | bytes 12488 | tf_op jit(solution)/shard_map/ppermute | solution.py:24
  20.7 6.0 %collective-permute-start.2 = (f32[8,132,2]{1,0,2:T(8,128)S(1)}, f32[8,132,2]{1,0,2:T(8,128)S(1)}, u32[]{:S(2)}, u32[]{:S(2)}) collective-permute-start(f32[8,132,2]{1,0,2:T(8,128)S(1)} %copy.11), channel_id=1, source_target_pairs={{0,4},{4,0},{1,5},{5,1},{2,6},{6,2},{3,7},{7,3},{8,12},{12,8},{9,1... | collective-permute-start | bytes 25352 | tf_op jit(solution)/shard_map/ppermute | solution.py:21
  21.1 6.0 %collective-permute-start.3 = (f32[8,132,2]{1,0,2:T(8,128)S(1)}, f32[8,132,2]{1,0,2:T(8,128)S(1)}, u32[]{:S(2)}, u32[]{:S(2)}) collective-permute-start(f32[8,132,2]{1,0,2:T(8,128)S(1)} %copy.12), channel_id=1, source_target_pairs={{4,0},{0,4},{5,1},{1,5},{6,2},{2,6},{7,3},{3,7},{12,8},{8,12},{13,... | collective-permute-start | bytes 25352 | tf_op jit(solution)/shard_map/ppermute | solution.py:24
  27.5 1.8 %copy-start = (bf16[2,8,130,514]{3,1,2,0:T(8,128)(2,1)S(1)}, bf16[2,8,130,514]{3,1,2,0:T(8,128)(2,1)}, u32[]{:S(2)}) copy-start(bf16[2,8,130,514]{3,1,2,0:T(8,128)(2,1)} %pad_maximum_fusion.14) | copy-start | bytes 6414724
  29.2 4.2 %copy-start.5 = (bf16[1,8,128,512]{3,2,1,0:T(8,128)(2,1)S(1)}, bf16[1,8,128,512]{3,2,1,0:T(8,128)(2,1)}, u32[]{:S(2)}) copy-start(bf16[1,8,128,512]{3,2,1,0:T(8,128)(2,1)} %get-tuple-element.7) | copy-start | bytes 3145732
  29.2 4.2 %copy-start.6 = (pred[128,512]{1,0:T(8,128)(4,1)S(1)}, pred[128,512]{1,0:T(8,128)(4,1)}, u32[]{:S(2)}) copy-start(pred[128,512]{1,0:T(8,128)(4,1)} %fusion.51) | copy-start | bytes 196612
  38.1 5.0 %collective-permute-start.8 = (f32[8,2,512]{2,0,1:T(8,128)S(1)}, f32[8,2,512]{2,0,1:T(8,128)S(1)}, u32[]{:S(2)}, u32[]{:S(2)}) collective-permute-start(f32[8,2,512]{2,0,1:T(8,128)S(1)} %get-tuple-element.14), channel_id=1, source_target_pairs={{0,8},{8,16},{16,24},{24,0},{1,9},{9,17},{17,25},{25,1},{2,10},{10... | collective-permute-start | bytes 98312 | tf_op jit(solution)/shard_map/ppermute | solution.py:21
  40.3 3.9 %collective-permute-start.9 = (f32[8,2,512]{2,0,1:T(8,128)S(1)}, f32[8,2,512]{2,0,1:T(8,128)S(1)}, u32[]{:S(2)}, u32[]{:S(2)}) collective-permute-start(f32[8,2,512]{2,0,1:T(8,128)S(1)} %get-tuple-element.15), channel_id=1, source_target_pairs={{8,0},{16,8},{24,16},{0,24},{9,1},{17,9},{25,17},{1,25},{10,2},{18... | collective-permute-start | bytes 98312 | tf_op jit(solution)/shard_map/ppermute | solution.py:24
  43.1 1.2 %copy-start.8 = (f32[8,2,512]{2,0,1:T(8,128)}, f32[8,2,512]{2,0,1:T(8,128)S(1)}, u32[]{:S(2)}) copy-start(f32[8,2,512]{2,0,1:T(8,128)S(1)} %collective-permute-done.8) | copy-start | bytes 98308
  44.3 0.6 copy-start.10
  45.2 16.2 %collective-permute-start.10 = (f32[8,132,2]{1,0,2:T(8,128)S(1)}, f32[8,132,2]{1,0,2:T(8,128)S(1)}, u32[]{:S(2)}, u32[]{:S(2)}) collective-permute-start(f32[8,132,2]{1,0,2:T(8,128)S(1)} %copy.25), channel_id=1, source_target_pairs={{0,4},{4,0},{1,5},{5,1},{2,6},{6,2},{3,7},{7,3},{8,12},{12,8},{9,1... | collective-permute-start | bytes 25352 | tf_op jit(solution)/shard_map/ppermute | solution.py:21
  45.6 16.2 %collective-permute-start.11 = (f32[8,132,2]{1,0,2:T(8,128)S(1)}, f32[8,132,2]{1,0,2:T(8,128)}, u32[]{:S(2)}, u32[]{:S(2)}) collective-permute-start(f32[8,132,2]{1,0,2:T(8,128)S(1)} %copy.26), channel_id=1, source_target_pairs={{4,0},{0,4},{5,1},{1,5},{6,2},{2,6},{7,3},{3,7},{12,8},{8,12},{13,... | collective-permute-start | bytes 25352 | tf_op jit(solution)/shard_map/ppermute | solution.py:24
  63.0 1.9 %copy-start.1 = (bf16[2,8,130,514]{3,1,2,0:T(8,128)(2,1)S(1)}, bf16[2,8,130,514]{3,1,2,0:T(8,128)(2,1)}, u32[]{:S(2)}) copy-start(bf16[2,8,130,514]{3,1,2,0:T(8,128)(2,1)} %pad_maximum_fusion.14) | copy-start | bytes 6414724
  63.0 1.9 %copy-start.9 = (f32[8,2,512]{2,0,1:T(8,128)S(1)}, f32[8,2,512]{2,0,1:T(8,128)}, u32[]{:S(2)}) copy-start(f32[8,2,512]{2,0,1:T(8,128)} %copy-done.8) | copy-start | bytes 98308
  63.0 1.9 %copy-start.11 = (f32[8,2,512]{2,0,1:T(8,128)S(1)}, f32[8,2,512]{2,0,1:T(8,128)}, u32[]{:S(2)}) copy-start(f32[8,2,512]{2,0,1:T(8,128)} %copy-done.10) | copy-start | bytes 98308
  64.9 4.3 %copy-start.4 = (bf16[1,8,128,512]{3,2,1,0:T(8,128)(2,1)S(1)}, bf16[1,8,128,512]{3,2,1,0:T(8,128)(2,1)}, u32[]{:S(2)}) copy-start(bf16[1,8,128,512]{3,2,1,0:T(8,128)(2,1)} %get-tuple-element.6) | copy-start | bytes 3145732
  64.9 4.3 %copy-start.7 = (pred[128,512]{1,0:T(8,128)(4,1)S(1)}, pred[128,512]{1,0:T(8,128)(4,1)}, u32[]{:S(2)}) copy-start(pred[128,512]{1,0:T(8,128)(4,1)} %fusion.51) | copy-start | bytes 196612
